TPU v7x, 32 devices: a whole 2x2x4 slice. The times are simulated.
32 devices in a mesh: seq: 8 (over y, x, core), head: 4 (over z).
Axes of the slice: x: 2, y: 2, z: 4, core: 2. Of those that a mesh axis runs over, the one named last changes fastest.
Arguments:
- queries: bfloat16 [8192, 2048], P('seq', 'head'), may hold values from -6 to 6
- keys: bfloat16 [8192, 2048], P('seq', 'head'), may hold values from -100 to 100
- values: bfloat16 [8192, 2048], P('seq', 'head'), may hold values from -16 to 16
- gates: float32 [8192, 16], P('seq', 'head'), may hold values from 0.05 to 1
- ridge: float32 [16], P('head'), may hold values from 0.25 to 4
- out_weight: bfloat16 [2048, 2048], P(None, 'head'), may hold values from -0.125 to 0.125
Outputs:
- partial_out: bfloat16 [4, 8192, 2048], P('head', 'seq')
All inputs are finite; a program needn't handle non-finite values.
Results may differ from a plain program's by a relative error of at most 0.0049.
Values may be sent and summed in bfloat16 or wider, within the bound.
A program may use at most 128 MiB of HBM per device.

v0:
```python
import functools

import jax
import jax.numpy as jnp
from jax import lax
from jax.experimental import pallas as pl
from jax.experimental.pallas import tpu as pltpu
from jax.sharding import PartitionSpec as P

HD = 128
SPAN = 128
ITERS = 8
EPS = 1e-06
f32 = jnp.float32
bf16 = jnp.bfloat16
VMEM_BYTES = 56 * 1024 * 1024


def dot(a, b):
    return jnp.dot(a, b, preferred_element_type=f32)


def two_terms(x):
    high = x.astype(bf16)
    return high, (x - high.astype(f32)).astype(bf16)


def inverse_norm(columns):
    return lax.rsqrt(jnp.sum(columns * columns, 0, keepdims=True) + EPS)


def block_sums(keys, values, gate_row):
    keys_t = keys.astype(f32).T
    s = inverse_norm(keys_t)
    w_value = gate_row * s
    w_key = w_value * s
    gram = dot(
        jnp.concatenate(two_terms(keys_t * w_key), 1), jnp.concatenate([keys, keys], 0)
    )
    moment = dot(
        jnp.concatenate(two_terms(keys_t * w_value), 1), jnp.concatenate([values, values], 0)
    )
    return gram, moment, keys_t, w_key, w_value


def totals_kernel(k_ref, v_ref, g_ref, out_ref):
    gram = jnp.zeros((HD, HD), f32)
    moment = jnp.zeros((HD, HD), f32)
    for c in range(k_ref.shape[0] // SPAN):
        rows = pl.ds(c * SPAN, SPAN)
        block_gram, block_moment, *_ = block_sums(k_ref[rows], v_ref[rows], g_ref[:, rows])
        gram += block_gram
        moment += block_moment
    out_ref[0, 0] = gram
    out_ref[1, 0] = moment


def solve_kernel(
    q_ref, k_ref, v_ref, g_ref, ridge_ref, table_ref, out_ref,
    system, weights, weights_value, moments, sol, res, direct,
):
    h = pl.program_id(0)
    me = lax.axis_index("seq")
    blocks = k_ref.shape[0] // SPAN
    row = lax.broadcasted_iota(jnp.int32, (HD, HD), 0)
    col = lax.broadcasted_iota(jnp.int32, (HD, HD), 1)
    causal = row <= col
    gram = jnp.where(row == col, ridge_ref[h], 0.0)
    moment = jnp.zeros((HD, HD), f32)
    for n in range(table_ref.shape[0]):
        lower = jnp.where(n < me, 1.0, 0.0).astype(f32)
        gram += lower * table_ref[n, 0, 0]
        moment += lower * table_ref[n, 1, 0]
    start = []
    for c in range(blocks):
        rows = pl.ds(c * SPAN, SPAN)
        block_gram, block_moment, keys_t, w_key, w_value = block_sums(
            k_ref[rows], v_ref[rows], g_ref[:, rows]
        )
        high, low = two_terms(gram)
        system[c] = jnp.concatenate([high, high, low, keys_t.astype(bf16)], 1)
        weights[c] = jnp.where(causal, jnp.broadcast_to(w_key, (SPAN, SPAN)).T, 0.0)
        weights_value[c] = jnp.where(causal, jnp.broadcast_to(w_value, (SPAN, SPAN)).T, 0.0)
        high, low = two_terms(moment)
        moments[c] = jnp.concatenate([high, high, low], 0)
        gram += block_gram
        moment += block_moment
        queries = q_ref[rows].astype(f32).T
        queries = queries * inverse_norm(queries)
        sol[c] = jnp.zeros((HD, SPAN), f32)
        res[c] = queries
        direct[c] = queries
        start.append(jnp.sum(queries * queries, 0, keepdims=True))

    def sweep(_, norms):
        after = []
        for c in range(blocks):
            rows = pl.ds(c * SPAN, SPAN)
            keys = k_ref[rows]
            d = direct[c]
            high, low = two_terms(d)
            corr = dot(jnp.concatenate([keys, keys], 1), jnp.concatenate([high, low], 0))
            corr = (corr * weights[c]).astype(bf16)
            image = dot(system[c], jnp.concatenate([high, low, high, corr], 0))
            now = norms[c]
            step = now / (jnp.sum(d * image, 0, keepdims=True) + EPS)
            sol[c] = sol[c] + step * d
            r = res[c] - step * image
            res[c] = r
            following = jnp.sum(r * r, 0, keepdims=True)
            direct[c] = r + following / (now + EPS) * d
            after.append(following)
        return tuple(after)

    lax.fori_loop(0, ITERS, sweep, tuple(start))
    for c in range(blocks):
        rows = pl.ds(c * SPAN, SPAN)
        keys = k_ref[rows]
        values = v_ref[rows]
        high, low = two_terms(sol[c])
        corr = dot(jnp.concatenate([keys, keys], 1), jnp.concatenate([high, low], 0))
        corr_high, corr_low = two_terms(corr * weights_value[c])
        left = jnp.concatenate([high, low, high, corr_high, corr_low], 0)
        right = jnp.concatenate([moments[c], values, values], 0)
        out_ref[rows] = lax.dot_general(
            left, right, (((0,), (0,)), ((), ())), preferred_element_type=f32
        ).astype(out_ref.dtype)


def project_kernel(r_ref, *refs):
    *pieces, out_ref = refs
    count = len(pieces)
    me = lax.axis_index("head")
    readout = r_ref[...]
    for shift, piece in enumerate(pieces):
        width = piece.shape[1]
        owner = lax.rem(me + count - shift, count)
        columns = pl.ds(pl.multiple_of(owner * width, width), width)
        out_ref[0, :, columns] = dot(readout, piece[...]).astype(out_ref.dtype)


def shards(n_seq, n_head, queries, keys, values, gates, ridge, out_weight):
    tokens, head_width = queries.shape
    heads = head_width // HD
    blocks = tokens // SPAN
    me = lax.axis_index("head")

    def rows_of(device):
        return lax.dynamic_slice_in_dim(out_weight, device * head_width, head_width, 0)

    pieces = [rows_of(me)]
    for shift in range(1, n_head):
        pairs = [(i, (i + shift) % n_head) for i in range(n_head)]
        pieces.append(lax.ppermute(rows_of(lax.rem(me + shift, n_head)), "head", pairs))

    gate_rows = gates.T[:, None]
    by_head = pl.BlockSpec((tokens, HD), lambda h: (0, h))
    gate_spec = pl.BlockSpec((None, 1, tokens), lambda h: (h, 0, 0))
    params = pltpu.CompilerParams(vmem_limit_bytes=VMEM_BYTES)
    tile = SPAN * HD * HD * 2
    totals = pl.pallas_call(
        totals_kernel,
        grid=(heads,),
        in_specs=[by_head, by_head, gate_spec],
        out_specs=pl.BlockSpec((2, 1, HD, HD), lambda h: (0, h, 0, 0)),
        out_shape=jax.ShapeDtypeStruct((2, heads, HD, HD), f32),
        compiler_params=params,
        cost_estimate=pl.CostEstimate(
            flops=heads * blocks * 4 * tile, bytes_accessed=tokens * head_width * 4, transcendentals=0
        ),
        name="totals",
    )(keys, values, gate_rows)
    table = lax.all_gather(totals, "seq", axis=0)
    state = pltpu.VMEM((blocks, HD, SPAN), f32)
    readout = pl.pallas_call(
        solve_kernel,
        grid=(heads,),
        in_specs=[
            by_head, by_head, by_head, gate_spec,
            pl.BlockSpec(memory_space=pltpu.SMEM),
            pl.BlockSpec((n_seq, 2, 1, HD, HD), lambda h: (0, 0, h, 0, 0)),
        ],
        out_specs=by_head,
        out_shape=jax.ShapeDtypeStruct((tokens, head_width), bf16),
        scratch_shapes=[
            pltpu.VMEM((blocks, HD, 4 * HD), bf16),
            state, state,
            pltpu.VMEM((blocks, 3 * HD, HD), bf16),
            state, state, state,
        ],
        compiler_params=params,
        cost_estimate=pl.CostEstimate(
            flops=heads * blocks * 54 * tile, bytes_accessed=tokens * head_width * 8, transcendentals=0
        ),
        name="solve",
    )(queries, keys, values, gate_rows, ridge, table)
    width = out_weight.shape[1]
    rows = 2 * SPAN
    whole = pl.BlockSpec((head_width, width), lambda i: (0, 0))
    return pl.pallas_call(
        project_kernel,
        grid=(tokens // rows,),
        in_specs=[pl.BlockSpec((rows, head_width), lambda i: (i, 0))] + [whole] * n_head,
        out_specs=pl.BlockSpec((1, rows, width * n_head), lambda i: (0, i, 0)),
        out_shape=jax.ShapeDtypeStruct((1, tokens, width * n_head), bf16),
        compiler_params=params,
        cost_estimate=pl.CostEstimate(
            flops=2 * tokens * head_width * width * n_head,
            bytes_accessed=tokens * width * n_head * 2,
            transcendentals=0,
        ),
        name="project",
    )(readout, *pieces)


def solution(mesh):
    return jax.shard_map(
        functools.partial(shards, mesh.shape["seq"], mesh.shape["head"]),
        mesh=mesh,
        in_specs=(
            P("seq", "head"),
            P("seq", "head"),
            P("seq", "head"),
            P("seq", "head"),
            P("head"),
            P(None, "head"),
        ),
        out_specs=P("head", "seq", None),
        check_vma=False,
    )
```

profile of v0, /device:TPU:13, one launch (start us, length us, event | category | flops | bytes accessed | tf_op | source)
XLA Modules:
  0.0 116.2 jit_solution(12984773233640785726)
XLA Ops:
  6.5 0.0 copy-start
  6.5 0.0 all-gather.3.cloned.1.call-start
  6.5 1.5 %broadcast_in_dim.3.g_ref = f32[4,1,1024]{2,1,0:T(1,128)} reshape(f32[4,1024]{1,0:T(4,128)} %bitcast.2) | data formatting | bytes 32768 | tf_op jit(solution)/shard_map/broadcast_in_dim | solution.py:156
  8.0 4.5 %totals.1 = f32[2,4,128,128]{3,2,1,0:T(8,128)} custom-call(bf16[1024,512]{1,0:T(8,128)(2,1)} %k_ref.3, bf16[1024,512]{1,0:T(8,128)(2,1)} %v_ref.3, f32[4,1,1024]{2,1,0:T(1,128)} %broadcast_in_dim.3.g_ref), custom_call_target="tpu_custom_call" | custom-call | flops 536870912 | bytes 2097152 | tf_op jit(solution)/shard_map/totals/pallas_call | solution.py:161
  12.5 0.0 all-gather.3.cloned.1.call-update
  12.6 0.0 copy-done
  12.6 1.2 %constant_dynamic-slice_fusion = (bf16[512,512]{1,0:T(8,128)(2,1)}, bf16[512,512]{1,0:T(8,128)(2,1)S(1)}, bf16[512,512]{1,0:T(8,128)(2,1)}, bf16[512,512]{1,0:T(8,128)(2,1)S(1)}) fusion(bf16[2048,512]{1,0:T(8,128)(2,1)S(1)} %copy-done, s32[]{:T(128)S(6)} %select_n.15, s32[]{:T(128)S(6)} %select_n.13, s32[]{:T(128)S(6)} %select_n.12, s32[]{:T(128)S(6)} %select_n.14), kind=kLoop, calls=%fused_computation | loop fusion | bytes 4194320 | tf_op jit(solution)/shard_map/dynamic_slice | solution.py:149
  13.8 0.2 collective-permute-start.2
  14.0 1.3 %collective-permute-start = (bf16[512,512]{1,0:T(8,128)(2,1)S(1)}, bf16[512,512]{1,0:T(8,128)(2,1)S(1)}, u32[]{:S(2)}, u32[]{:S(2)}) collective-permute-start(bf16[512,512]{1,0:T(8,128)(2,1)S(1)} %get-tuple-element.6), channel_id=1, source_target_pairs={{0,1},{1,2},{2,3},{3,0},{4,5},{5,6},{6,7},{7,4},{8,9},{9,10},{10,1... | collective-permute-start | bytes 1572872 | tf_op jit(solution)/shard_map/ppermute | solution.py:154
  15.3 4.1 %collective-permute-start.1 = (bf16[512,512]{1,0:T(8,128)(2,1)S(1)}, bf16[512,512]{1,0:T(8,128)(2,1)S(1)}, u32[]{:S(2)}, u32[]{:S(2)}) collective-permute-start(bf16[512,512]{1,0:T(8,128)(2,1)S(1)} %get-tuple-element.8), channel_id=1, source_target_pairs={{0,2},{1,3},{2,0},{3,1},{4,6},{5,7},{6,4},{7,5},{8,10},{9,11},{10,... | collective-permute-start | bytes 1572872 | tf_op jit(solution)/shard_map/ppermute | solution.py:154
  19.4 31.3 %all-gather.3.cloned.1.call-done = f32[16,4,128,128]{3,2,1,0:T(8,128)} async-done(((f32[2,4,128,128]{3,2,1,0:T(8,128)}), f32[16,4,128,128]{3,2,1,0:T(8,128)}) %all-gather.3.cloned.1.call-update) | async-done | bytes 4194320 | tf_op jit(solution)/shard_map/all_gather | solution.py:173
  50.6 51.5 %solve.1.r_ref = bf16[1024,512]{1,0:T(8,128)(2,1)} custom-call(bf16[1024,512]{1,0:T(8,128)(2,1)} %q_ref.1, bf16[1024,512]{1,0:T(8,128)(2,1)} %k_ref.3, bf16[1024,512]{1,0:T(8,128)(2,1)} %v_ref.3, f32[4,1,1024]{2,1,0:T(1,128)} %broadcast_in_dim.3.g_ref, f32[4]{0:T(128)} %ridge_ref.1, f32[8,2,4,128,128]{4,3,2,1,0:T(8,128)} %bitcast.3), custom_call_target="tpu_custom_call" | custom-call | flops 7247757312 | bytes 4194304 | tf_op jit(solution)/shard_map/solve/pallas_call | solution.py:175
  102.2 0.0 collective-permute-done.2.refs_3_
  102.2 0.0 copy-start.1
  102.2 0.0 collective-permute-done.refs_1_
  102.2 0.0 copy-start.2
  102.2 0.0 collective-permute-done.1.refs_2_
  102.2 0.0 copy-start.3
  102.2 0.8 copy-done.1
  103.0 0.1 copy-done.2
  103.2 0.2 copy-done.3
  103.3 6.1 %project.1 = bf16[1,1024,2048]{2,1,0:T(8,128)(2,1)} custom-call(bf16[1024,512]{1,0:T(8,128)(2,1)} %solve.1.r_ref, bf16[512,512]{1,0:T(8,128)(2,1)} %get-tuple-element.7.refs_0_, bf16[512,512]{1,0:T(8,128)(2,1)} %copy-done.2, bf16[512,512]{1,0:T(8,128)(2,1)} %copy-done.3, bf16[512,512]{1,0:T(8,128)(2,1)} %copy-done.1), custom_call_target="tpu_custom_call" | custom-call | flops 2147483648 | bytes 4194304 | tf_op jit(solution)/shard_map/project/pallas_call | solution.py:200
Async XLA Ops:
  6.5 6.0 %copy-start = (bf16[2048,512]{1,0:T(8,128)(2,1)S(1)}, bf16[2048,512]{1,0:T(8,128)(2,1)}, u32[]{:S(2)}) copy-start(bf16[2048,512]{1,0:T(8,128)(2,1)} %param.11) | copy-start | bytes 6291460
  6.5 44.1 %all-gather.3.cloned.1.call-start = ((), (), s32[]{:S(2)}) async-start(), calls=%async_computation | async-start | bytes 4718592 | tf_op jit(solution)/shard_map/all_gather | solution.py:173
  13.8 88.4 %collective-permute-start.2 = (bf16[512,512]{1,0:T(8,128)(2,1)}, bf16[512,512]{1,0:T(8,128)(2,1)S(1)}, u32[]{:S(2)}, u32[]{:S(2)}) collective-permute-start(bf16[512,512]{1,0:T(8,128)(2,1)} %get-tuple-element.5), channel_id=1, source_target_pairs={{0,3},{1,0},{2,1},{3,2},{4,7},{5,4},{6,5},{7,6},{8,11},{9,8},{10,9... | collective-permute-start | bytes 1572872 | tf_op jit(solution)/shard_map/ppermute | solution.py:154
  14.0 88.2 %collective-permute-start = (bf16[512,512]{1,0:T(8,128)(2,1)S(1)}, bf16[512,512]{1,0:T(8,128)(2,1)S(1)}, u32[]{:S(2)}, u32[]{:S(2)}) collective-permute-start(bf16[512,512]{1,0:T(8,128)(2,1)S(1)} %get-tuple-element.6), channel_id=1, source_target_pairs={{0,1},{1,2},{2,3},{3,0},{4,5},{5,6},{6,7},{7,4},{8,9},{9,10},{10,1... | collective-permute-start | bytes 1572872 | tf_op jit(solution)/shard_map/ppermute | solution.py:154
  15.3 86.9 %collective-permute-start.1 = (bf16[512,512]{1,0:T(8,128)(2,1)S(1)}, bf16[512,512]{1,0:T(8,128)(2,1)S(1)}, u32[]{:S(2)}, u32[]{:S(2)}) collective-permute-start(bf16[512,512]{1,0:T(8,128)(2,1)S(1)} %get-tuple-element.8), channel_id=1, source_target_pairs={{0,2},{1,3},{2,0},{3,1},{4,6},{5,7},{6,4},{7,5},{8,10},{9,11},{10,... | collective-permute-start | bytes 1572872 | tf_op jit(solution)/shard_map/ppermute | solution.py:154
  102.2 0.8 copy-start.1
  102.2 1.0 copy-start.2
  102.2 1.1 copy-start.3
Sparse Core Ops, SparseCore 0:
  12.7 37.9 all-gather.2
where the time goes:
time: 118 us; the launch traced here: 116 us
  Pallas kernels  62.1 us (53%)
  waiting for transfers between devices  31.3 us (27%)
  between operations  13.5 us (11%)
  starting transfers between devices  5.58 us (5%)
  local copies, waits for them, and re-layouts  3.81 us (3%)
    pallas_call x1, Pallas kernels, shards(): pl.pallas_call(solve_kernel, grid=(heads,), in_specs=[by_head, by_head, b...  51.5 us
    all_gather x1, waiting for transfers between devices, shards(): table = lax.all_gather(totals, 'seq', axis=0)  31.3 us
    pallas_call x1, Pallas kernels, shards(): pl.pallas_call(project_kernel, grid=(tokens // rows,), in_specs=[pl.Block...  6.08 us
    ppermute x3, starting transfers between devices, shards(): lax.ppermute(rows_of(lax.rem(me + shift, n_head)), 'head', pairs)  5.58 us
    pallas_call x1, Pallas kernels, shards(): pl.pallas_call(totals_kernel, grid=(heads,), in_specs=[by_head, by_head,...  4.49 us
  transfers between devices with their start and end apart: 4, of which 1 were waited for; matrix products, arithmetic and copies ran while one was open for 1% of the time, Pallas kernels for 44%

commit v1 on v0

--- a/solution.py
+++ b/solution.py
@@ -29,10 +29,10 @@
     return lax.rsqrt(jnp.sum(columns * columns, 0, keepdims=True) + EPS)
 
 
-def block_sums(keys, values, gate_row):
+def block_sums(keys, values, gate):
     keys_t = keys.astype(f32).T
     s = inverse_norm(keys_t)
-    w_value = gate_row * s
+    w_value = gate * s
     w_key = w_value * s
     gram = dot(
         jnp.concatenate(two_terms(keys_t * w_key), 1), jnp.concatenate([keys, keys], 0)
@@ -43,42 +43,119 @@
     return gram, moment, keys_t, w_key, w_value
 
 
-def totals_kernel(k_ref, v_ref, g_ref, out_ref):
-    gram = jnp.zeros((HD, HD), f32)
-    moment = jnp.zeros((HD, HD), f32)
-    for c in range(k_ref.shape[0] // SPAN):
-        rows = pl.ds(c * SPAN, SPAN)
-        block_gram, block_moment, *_ = block_sums(k_ref[rows], v_ref[rows], g_ref[:, rows])
-        gram += block_gram
-        moment += block_moment
-    out_ref[0, 0] = gram
-    out_ref[1, 0] = moment
+def gate_row(g_ref, h, rows):
+    gates = g_ref[:, rows]
+    return jnp.sum(
+        jnp.where(lax.broadcasted_iota(jnp.int32, gates.shape, 0) == h, gates, 0.0), 0, keepdims=True
+    )
+
+
+def prefix_kernel(
+    n_seq, k_ref, v_ref, g_ref, out_ref,
+    own, mate, chip_sum, slots, give, final, mate_sems, send_sems, recv_sems, final_sems,
+):
+    heads = out_ref.shape[0]
+    half = heads // 2
+    pairs = n_seq // 2
+    me = lax.axis_index("seq")
+    side = lax.rem(me, 2)
+    pair = me // 2
+    mate_at = {"seq": me + 1 - 2 * side}
+    mine = side * half
+    others = (1 - side) * half
+
+    barrier = pltpu.get_barrier_semaphore()
+    pl.semaphore_signal(barrier, inc=1, device_id=mate_at, device_id_type=pl.DeviceIdType.MESH)
+    for off in range(1, pairs):
+        target = {"seq": lax.rem(pair + off, pairs) * 2 + side}
+        pl.semaphore_signal(barrier, inc=1, device_id=target, device_id_type=pl.DeviceIdType.MESH)
+
+    def sum_head(h):
+        gram = jnp.zeros((HD, HD), f32)
+        moment = jnp.zeros((HD, HD), f32)
+        columns = pl.ds(pl.multiple_of(h * HD, HD), HD)
+        for c in range(k_ref.shape[0] // SPAN):
+            rows = pl.ds(c * SPAN, SPAN)
+            block_gram, block_moment, *_ = block_sums(
+                k_ref[rows, columns], v_ref[rows, columns], gate_row(g_ref, h, rows)
+            )
+            gram += block_gram
+            moment += block_moment
+        own[h, 0] = gram
+        own[h, 1] = moment
+
+    for j in range(half):
+        sum_head(others + j)
+    pl.semaphore_wait(barrier, pairs)
+    to_mate = pltpu.make_async_remote_copy(
+        src_ref=own.at[pl.ds(others, half)], dst_ref=mate,
+        send_sem=mate_sems.at[0], recv_sem=mate_sems.at[1],
+        device_id=mate_at, device_id_type=pl.DeviceIdType.MESH,
+    )
+    to_mate.start()
+    for j in range(half):
+        sum_head(mine + j)
+    to_mate.wait()
+    chip_sum[...] = own[pl.ds(mine, half)] + mate[...]
+
+    def to_later(off):
+        target = {"seq": lax.rem(pair + off, pairs) * 2 + side}
+        return pltpu.make_async_remote_copy(
+            src_ref=chip_sum, dst_ref=slots.at[off - 1],
+            send_sem=send_sems.at[off - 1], recv_sem=recv_sems.at[off - 1],
+            device_id=target, device_id_type=pl.DeviceIdType.MESH,
+        )
+
+    for off in range(1, pairs):
+        @pl.when(pair + off < pairs)
+        def _():
+            to_later(off).start()
+
+    give[...] = jnp.zeros(give.shape, f32)
+    for off in range(1, pairs):
+        @pl.when(pair >= off)
+        def _():
+            to_later(off).wait_recv()
+            give[...] = give[...] + slots[off - 1]
+
+    out_ref[pl.ds(mine, half)] = give[...] + side.astype(f32) * mate[...]
+    give[...] = give[...] + (1 - side).astype(f32) * own[pl.ds(mine, half)]
+    back = pltpu.make_async_remote_copy(
+        src_ref=give, dst_ref=final,
+        send_sem=final_sems.at[0], recv_sem=final_sems.at[1],
+        device_id=mate_at, device_id_type=pl.DeviceIdType.MESH,
+    )
+    back.start()
+    back.wait()
+    out_ref[pl.ds(others, half)] = final[...]
+    for off in range(1, pairs):
+        @pl.when(pair + off < pairs)
+        def _():
+            to_later(off).wait_send()
 
 
 def solve_kernel(
-    q_ref, k_ref, v_ref, g_ref, ridge_ref, table_ref, out_ref,
-    system, weights, weights_value, moments, sol, res, direct,
+    q_ref, k_ref, v_ref, g_ref, ridge_ref, prior_ref, out_ref,
+    first, second, weights, weights_value, moments, sol, res, direct,
 ):
     h = pl.program_id(0)
-    me = lax.axis_index("seq")
     blocks = k_ref.shape[0] // SPAN
     row = lax.broadcasted_iota(jnp.int32, (HD, HD), 0)
     col = lax.broadcasted_iota(jnp.int32, (HD, HD), 1)
     causal = row <= col
-    gram = jnp.where(row == col, ridge_ref[h], 0.0)
-    moment = jnp.zeros((HD, HD), f32)
-    for n in range(table_ref.shape[0]):
-        lower = jnp.where(n < me, 1.0, 0.0).astype(f32)
-        gram += lower * table_ref[n, 0, 0]
-        moment += lower * table_ref[n, 1, 0]
+    gram = jnp.where(row == col, ridge_ref[h], 0.0) + prior_ref[0]
+    moment = prior_ref[1]
     start = []
     for c in range(blocks):
         rows = pl.ds(c * SPAN, SPAN)
         block_gram, block_moment, keys_t, w_key, w_value = block_sums(
-            k_ref[rows], v_ref[rows], g_ref[:, rows]
+            k_ref[rows], v_ref[rows], gate_row(g_ref, h, rows)
         )
         high, low = two_terms(gram)
-        system[c] = jnp.concatenate([high, high, low, keys_t.astype(bf16)], 1)
+        keys = k_ref[rows]
+        first[c, :HD] = jnp.concatenate([keys, keys], 1)
+        first[c, HD:] = jnp.concatenate([high, high], 1)
+        second[c] = jnp.concatenate([low, keys_t.astype(bf16)], 1)
         weights[c] = jnp.where(causal, jnp.broadcast_to(w_key, (SPAN, SPAN)).T, 0.0)
         weights_value[c] = jnp.where(causal, jnp.broadcast_to(w_value, (SPAN, SPAN)).T, 0.0)
         high, low = two_terms(moment)
@@ -95,13 +172,11 @@
     def sweep(_, norms):
         after = []
         for c in range(blocks):
-            rows = pl.ds(c * SPAN, SPAN)
-            keys = k_ref[rows]
             d = direct[c]
             high, low = two_terms(d)
-            corr = dot(jnp.concatenate([keys, keys], 1), jnp.concatenate([high, low], 0))
-            corr = (corr * weights[c]).astype(bf16)
-            image = dot(system[c], jnp.concatenate([high, low, high, corr], 0))
+            both = dot(first[c], jnp.concatenate([high, low], 0))
+            corr = (both[:HD] * weights[c]).astype(bf16)
+            image = both[HD:] + dot(second[c], jnp.concatenate([high, corr], 0))
             now = norms[c]
             step = now / (jnp.sum(d * image, 0, keepdims=True) + EPS)
             sol[c] = sol[c] + step * d
@@ -153,24 +228,38 @@
         pairs = [(i, (i + shift) % n_head) for i in range(n_head)]
         pieces.append(lax.ppermute(rows_of(lax.rem(me + shift, n_head)), "head", pairs))
 
-    gate_rows = gates.T[:, None]
+    gate_rows = gates.T
     by_head = pl.BlockSpec((tokens, HD), lambda h: (0, h))
-    gate_spec = pl.BlockSpec((None, 1, tokens), lambda h: (h, 0, 0))
+    gate_spec = pl.BlockSpec((heads, tokens), lambda h: (0, 0))
     params = pltpu.CompilerParams(vmem_limit_bytes=VMEM_BYTES)
     tile = SPAN * HD * HD * 2
-    totals = pl.pallas_call(
-        totals_kernel,
-        grid=(heads,),
-        in_specs=[by_head, by_head, gate_spec],
-        out_specs=pl.BlockSpec((2, 1, HD, HD), lambda h: (0, h, 0, 0)),
-        out_shape=jax.ShapeDtypeStruct((2, heads, HD, HD), f32),
-        compiler_params=params,
+    half = heads // 2
+    pairs = n_seq // 2
+    part = pltpu.VMEM((half, 2, HD, HD), f32)
+    in_vmem = pl.BlockSpec(memory_space=pltpu.VMEM)
+    prior = pl.pallas_call(
+        functools.partial(prefix_kernel, n_seq),
+        in_specs=[in_vmem] * 3,
+        out_specs=in_vmem,
+        out_shape=jax.ShapeDtypeStruct((heads, 2, HD, HD), f32),
+        scratch_shapes=[
+            pltpu.VMEM((heads, 2, HD, HD), f32),
+            part, part,
+            pltpu.VMEM((pairs - 1, half, 2, HD, HD), f32),
+            part, part,
+            pltpu.SemaphoreType.DMA((2,)),
+            pltpu.SemaphoreType.DMA((pairs - 1,)),
+            pltpu.SemaphoreType.DMA((pairs - 1,)),
+            pltpu.SemaphoreType.DMA((2,)),
+        ],
+        compiler_params=pltpu.CompilerParams(
+            vmem_limit_bytes=VMEM_BYTES, collective_id=0, has_side_effects=True
+        ),
         cost_estimate=pl.CostEstimate(
             flops=heads * blocks * 4 * tile, bytes_accessed=tokens * head_width * 4, transcendentals=0
         ),
-        name="totals",
+        name="prefix",
     )(keys, values, gate_rows)
-    table = lax.all_gather(totals, "seq", axis=0)
     state = pltpu.VMEM((blocks, HD, SPAN), f32)
     readout = pl.pallas_call(
         solve_kernel,
@@ -178,12 +267,13 @@
         in_specs=[
             by_head, by_head, by_head, gate_spec,
             pl.BlockSpec(memory_space=pltpu.SMEM),
-            pl.BlockSpec((n_seq, 2, 1, HD, HD), lambda h: (0, 0, h, 0, 0)),
+            pl.BlockSpec((None, 2, HD, HD), lambda h: (h, 0, 0, 0)),
         ],
         out_specs=by_head,
         out_shape=jax.ShapeDtypeStruct((tokens, head_width), bf16),
         scratch_shapes=[
-            pltpu.VMEM((blocks, HD, 4 * HD), bf16),
+            pltpu.VMEM((blocks, 2 * HD, 2 * HD), bf16),
+            pltpu.VMEM((blocks, HD, 2 * HD), bf16),
             state, state,
             pltpu.VMEM((blocks, 3 * HD, HD), bf16),
             state, state, state,
@@ -193,7 +283,7 @@
             flops=heads * blocks * 54 * tile, bytes_accessed=tokens * head_width * 8, transcendentals=0
         ),
         name="solve",
-    )(queries, keys, values, gate_rows, ridge, table)
+    )(queries, keys, values, gate_rows, ridge, prior)
     width = out_weight.shape[1]
     rows = 2 * SPAN
     whole = pl.BlockSpec((head_width, width), lambda i: (0, 0))

time: 118 us -> 105 us (0.89); the launches traced: 116 us -> 105 us
  Pallas kernels: 62.1 us -> 95.8 us
  waiting for transfers between devices: 31.3 us -> 0.01 us
  between operations: 13.5 us -> 0.05 us
    all_gather x1 -> x0, waiting for transfers between devices: 31.3 us -> none  [shards(): table = lax.all_gather(totals, 'seq', axis=0)]
    pallas_call x1, Pallas kernels: 4.49 us -> 21.7 us  [shards(): pl.pallas_call(functools.partial(prefix_kernel, n_seq), in_specs=[in_vmem...]
    pallas_call x1, Pallas kernels: 51.5 us -> 68 us  [shards(): pl.pallas_call(solve_kernel, grid=(heads,), in_specs=[by_head, by_head, b...]
    broadcast_in_dim x1 -> x0, local copies, waits for them, and re-layouts: 1.48 us -> none  [shards(): gate_rows = gates.T[:, None]]
    dynamic_slice x1, local copies, waits for them, and re-layouts: 1.22 us -> 2.45 us  [rows_of(): lax.dynamic_slice_in_dim(out_weight, device * head_width, head_width, 0)]
  transfers between devices with their start and end apart: 4 -> 3, of which waited for: 1 -> 0; matrix products, arithmetic and copies ran while one was open for 1% -> 0% of each run, Pallas kernels for 44% -> 85%
where the time goes in v1:
time: 105 us
  Pallas kernels  95.8 us (91%)
  starting transfers between devices  5.57 us (5%)
  local copies, waits for them, and re-layouts  3.55 us (3%)
    pallas_call x1, Pallas kernels, shards(): pl.pallas_call(solve_kernel, grid=(heads,), in_specs=[by_head, by_head, b...  68 us
    pallas_call x1, Pallas kernels, shards(): pl.pallas_call(functools.partial(prefix_kernel, n_seq), in_specs=[in_vmem...  21.7 us
    pallas_call x1, Pallas kernels, shards(): pl.pallas_call(project_kernel, grid=(tokens // rows,), in_specs=[pl.Block...  6.08 us
    ppermute x3, starting transfers between devices, shards(): lax.ppermute(rows_of(lax.rem(me + shift, n_head)), 'head', pairs)  5.57 us
    dynamic_slice x1, local copies, waits for them, and re-layouts, rows_of(): lax.dynamic_slice_in_dim(out_weight, device * head_width, head_width, 0)  2.45 us
  transfers between devices with their start and end apart: 3, of which 0 were waited for; matrix products, arithmetic and copies ran while one was open for 0% of the time, Pallas kernels for 85%

profile of v1, /device:TPU:13, one launch (start us, length us, event | category | flops | bytes accessed | tf_op | source)
XLA Modules:
  0.0 104.9 jit_solution(4285271698149243427)
XLA Ops:
  0.0 2.5 %constant_dynamic-slice_fusion = (bf16[512,512]{1,0:T(8,128)(2,1)S(1)}, bf16[512,512]{1,0:T(8,128)(2,1)S(1)}, bf16[512,512]{1,0:T(8,128)(2,1)}, bf16[512,512]{1,0:T(8,128)(2,1)S(1)}) fusion(bf16[2048,512]{1,0:T(8,128)(2,1)} %param.11, s32[]{:T(128)S(6)} %select_n.15, s32[]{:T(128)S(6)} %select_n.13, s32[]{:T(128)S(6)} %select_n.12, s32[]{:T(128)S(6)} %select_n.14), kind=kLoop, calls=%fused_computation | loop fusion | bytes 4194320 | tf_op jit(solution)/shard_map/dynamic_slice | solution.py:224
  2.5 0.2 collective-permute-start.2
  2.6 1.3 %collective-permute-start = (bf16[512,512]{1,0:T(8,128)(2,1)S(1)}, bf16[512,512]{1,0:T(8,128)(2,1)S(1)}, u32[]{:S(2)}, u32[]{:S(2)}) collective-permute-start(bf16[512,512]{1,0:T(8,128)(2,1)S(1)} %get-tuple-element.6), channel_id=1, source_target_pairs={{0,1},{1,2},{2,3},{3,0},{4,5},{5,6},{6,7},{7,4},{8,9},{9,10},{10,1... | collective-permute-start | bytes 1572872 | tf_op jit(solution)/shard_map/ppermute | solution.py:229
  3.9 4.1 %collective-permute-start.1 = (bf16[512,512]{1,0:T(8,128)(2,1)S(1)}, bf16[512,512]{1,0:T(8,128)(2,1)S(1)}, u32[]{:S(2)}, u32[]{:S(2)}) collective-permute-start(bf16[512,512]{1,0:T(8,128)(2,1)S(1)} %get-tuple-element.8), channel_id=1, source_target_pairs={{0,2},{1,3},{2,0},{3,1},{4,6},{5,7},{6,4},{7,5},{8,10},{9,11},{10,... | collective-permute-start | bytes 1572872 | tf_op jit(solution)/shard_map/ppermute | solution.py:229
  8.0 21.7 %prefix.1.prior_ref = f32[4,2,128,128]{3,2,1,0:T(8,128)} custom-call(bf16[1024,512]{1,0:T(8,128)(2,1)} %k_ref.3, bf16[1024,512]{1,0:T(8,128)(2,1)} %v_ref.3, f32[4,1024]{1,0:T(4,128)} %bitcast.1), custom_call_target="tpu_custom_call" | custom-call | flops 536870912 | bytes 2097152 | tf_op jit(solution)/shard_map/prefix/pallas_call | solution.py:240
  29.7 68.0 %solve.1.r_ref = bf16[1024,512]{1,0:T(8,128)(2,1)} custom-call(bf16[1024,512]{1,0:T(8,128)(2,1)} %q_ref.1, bf16[1024,512]{1,0:T(8,128)(2,1)} %k_ref.3, bf16[1024,512]{1,0:T(8,128)(2,1)} %v_ref.3, f32[4,1024]{1,0:T(4,128)} %bitcast.2, f32[4]{0:T(128)} %ridge_ref.1, f32[4,2,128,128]{3,2,1,0:T(8,128)} %prefix.1.prior_ref), custom_call_target="tpu_custom_call" | custom-call | flops 7247757312 | bytes 4194304 | tf_op jit(solution)/shard_map/solve/pallas_call | solution.py:264
  97.7 0.0 collective-permute-done.2.refs_3_
  97.7 0.0 copy-start
  97.7 0.0 collective-permute-done.refs_1_
  97.7 0.0 copy-start.1
  97.7 0.0 collective-permute-done.1.refs_2_
  97.8 0.0 copy-start.2
  97.8 0.8 copy-done
  98.5 0.2 copy-done.1
  98.7 0.2 copy-done.2
  98.9 6.1 %project.1 = bf16[1,1024,2048]{2,1,0:T(8,128)(2,1)} custom-call(bf16[1024,512]{1,0:T(8,128)(2,1)} %solve.1.r_ref, bf16[512,512]{1,0:T(8,128)(2,1)} %get-tuple-element.7.refs_0_, bf16[512,512]{1,0:T(8,128)(2,1)} %copy-done.1, bf16[512,512]{1,0:T(8,128)(2,1)} %copy-done.2, bf16[512,512]{1,0:T(8,128)(2,1)} %copy-done), custom_call_target="tpu_custom_call" | custom-call | flops 2147483648 | bytes 4194304 | tf_op jit(solution)/shard_map/project/pallas_call | solution.py:290
Async XLA Ops:
  2.5 95.3 %collective-permute-start.2 = (bf16[512,512]{1,0:T(8,128)(2,1)S(1)}, bf16[512,512]{1,0:T(8,128)(2,1)S(1)}, u32[]{:S(2)}, u32[]{:S(2)}) collective-permute-start(bf16[512,512]{1,0:T(8,128)(2,1)S(1)} %get-tuple-element.5), channel_id=1, source_target_pairs={{0,3},{1,0},{2,1},{3,2},{4,7},{5,4},{6,5},{7,6},{8,11},{9,8},{10,9... | collective-permute-start | bytes 1572872 | tf_op jit(solution)/shard_map/ppermute | solution.py:229
  2.6 95.1 %collective-permute-start = (bf16[512,512]{1,0:T(8,128)(2,1)S(1)}, bf16[512,512]{1,0:T(8,128)(2,1)S(1)}, u32[]{:S(2)}, u32[]{:S(2)}) collective-permute-start(bf16[512,512]{1,0:T(8,128)(2,1)S(1)} %get-tuple-element.6), channel_id=1, source_target_pairs={{0,1},{1,2},{2,3},{3,0},{4,5},{5,6},{6,7},{7,4},{8,9},{9,10},{10,1... | collective-permute-start | bytes 1572872 | tf_op jit(solution)/shard_map/ppermute | solution.py:229
  3.9 93.8 %collective-permute-start.1 = (bf16[512,512]{1,0:T(8,128)(2,1)S(1)}, bf16[512,512]{1,0:T(8,128)(2,1)S(1)}, u32[]{:S(2)}, u32[]{:S(2)}) collective-permute-start(bf16[512,512]{1,0:T(8,128)(2,1)S(1)} %get-tuple-element.8), channel_id=1, source_target_pairs={{0,2},{1,3},{2,0},{3,1},{4,6},{5,7},{6,4},{7,5},{8,10},{9,11},{10,... | collective-permute-start | bytes 1572872 | tf_op jit(solution)/shard_map/ppermute | solution.py:229
  97.7 0.8 copy-start
  97.7 1.0 copy-start.1
  97.8 1.1 %copy-start.2 = (bf16[512,512]{1,0:T(8,128)(2,1)}, bf16[512,512]{1,0:T(8,128)(2,1)S(1)}, u32[]{:S(2)}) copy-start(bf16[512,512]{1,0:T(8,128)(2,1)S(1)} %collective-permute-done.1.refs_2_) | copy-start | bytes 1572868

commit v2 on v1

--- a/solution.py
+++ b/solution.py
@@ -137,6 +137,7 @@
 def solve_kernel(
     q_ref, k_ref, v_ref, g_ref, ridge_ref, prior_ref, out_ref,
     first, second, weights, weights_value, moments, sol, res, direct,
+    terms, corrs, images,
 ):
     h = pl.program_id(0)
     blocks = k_ref.shape[0] // SPAN
@@ -153,9 +154,8 @@
         )
         high, low = two_terms(gram)
         keys = k_ref[rows]
-        first[c, :HD] = jnp.concatenate([keys, keys], 1)
-        first[c, HD:] = jnp.concatenate([high, high], 1)
-        second[c] = jnp.concatenate([low, keys_t.astype(bf16)], 1)
+        first[c] = jnp.concatenate([keys, keys], 1)
+        second[c] = jnp.concatenate([high, high, low, keys_t.astype(bf16)], 1)
         weights[c] = jnp.where(causal, jnp.broadcast_to(w_key, (SPAN, SPAN)).T, 0.0)
         weights_value[c] = jnp.where(causal, jnp.broadcast_to(w_value, (SPAN, SPAN)).T, 0.0)
         high, low = two_terms(moment)
@@ -172,11 +172,18 @@
     def sweep(_, norms):
         after = []
         for c in range(blocks):
+            high, low = two_terms(direct[c])
+            terms[c, :HD] = high
+            terms[c, HD:] = low
+        for c in range(blocks):
+            corr = dot(first[c], terms[c])
+            corrs[c] = (corr * weights[c]).astype(bf16)
+        for c in range(blocks):
+            both = terms[c]
+            images[c] = dot(second[c], jnp.concatenate([both, both[:HD], corrs[c]], 0))
+        for c in range(blocks):
             d = direct[c]
-            high, low = two_terms(d)
-            both = dot(first[c], jnp.concatenate([high, low], 0))
-            corr = (both[:HD] * weights[c]).astype(bf16)
-            image = both[HD:] + dot(second[c], jnp.concatenate([high, corr], 0))
+            image = images[c]
             now = norms[c]
             step = now / (jnp.sum(d * image, 0, keepdims=True) + EPS)
             sol[c] = sol[c] + step * d
@@ -272,11 +279,14 @@
         out_specs=by_head,
         out_shape=jax.ShapeDtypeStruct((tokens, head_width), bf16),
         scratch_shapes=[
-            pltpu.VMEM((blocks, 2 * HD, 2 * HD), bf16),
             pltpu.VMEM((blocks, HD, 2 * HD), bf16),
+            pltpu.VMEM((blocks, HD, 4 * HD), bf16),
             state, state,
             pltpu.VMEM((blocks, 3 * HD, HD), bf16),
             state, state, state,
+            pltpu.VMEM((blocks, 2 * HD, SPAN), bf16),
+            pltpu.VMEM((blocks, HD, SPAN), bf16),
+            state,
         ],
         compiler_params=params,
         cost_estimate=pl.CostEstimate(

time: 105 us -> 74.5 us (0.71)
  Pallas kernels: 95.8 us -> 65 us
    pallas_call x1, Pallas kernels: 68 us -> 37.3 us  [shards(): pl.pallas_call(solve_kernel, grid=(heads,), in_specs=[by_head, by_head, b...]
  transfers between devices with their start and end apart: 3 -> 3, of which waited for: 0 -> 0; matrix products, arithmetic and copies ran while one was open for 0% -> 0% of each run, Pallas kernels for 85% -> 79%
where the time goes in v2:
time: 74.5 us; the launch traced here: 74.2 us
  Pallas kernels  65 us (87%)
  starting transfers between devices  5.57 us (7%)
  local copies, waits for them, and re-layouts  3.55 us (5%)
    pallas_call x1, Pallas kernels, shards(): pl.pallas_call(solve_kernel, grid=(heads,), in_specs=[by_head, by_head, b...  37.3 us
    pallas_call x1, Pallas kernels, shards(): pl.pallas_call(functools.partial(prefix_kernel, n_seq), in_specs=[in_vmem...  21.7 us
    pallas_call x1, Pallas kernels, shards(): pl.pallas_call(project_kernel, grid=(tokens // rows,), in_specs=[pl.Block...  6.08 us
    ppermute x3, starting transfers between devices, shards(): lax.ppermute(rows_of(lax.rem(me + shift, n_head)), 'head', pairs)  5.57 us
    dynamic_slice x1, local copies, waits for them, and re-layouts, rows_of(): lax.dynamic_slice_in_dim(out_weight, device * head_width, head_width, 0)  2.45 us
  transfers between devices with their start and end apart: 3, of which 0 were waited for; matrix products, arithmetic and copies ran while one was open for 0% of the time, Pallas kernels for 79%

profile of v2, /device:TPU:13, one launch (start us, length us, event | category | flops | bytes accessed | tf_op | source)
XLA Modules:
  0.0 74.2 jit_solution(967963000142451429)
XLA Ops:
  0.0 2.5 %constant_dynamic-slice_fusion = (bf16[512,512]{1,0:T(8,128)(2,1)S(1)}, bf16[512,512]{1,0:T(8,128)(2,1)S(1)}, bf16[512,512]{1,0:T(8,128)(2,1)}, bf16[512,512]{1,0:T(8,128)(2,1)S(1)}) fusion(bf16[2048,512]{1,0:T(8,128)(2,1)} %param.11, s32[]{:T(128)S(6)} %select_n.15, s32[]{:T(128)S(6)} %select_n.13, s32[]{:T(128)S(6)} %select_n.12, s32[]{:T(128)S(6)} %select_n.14), kind=kLoop, calls=%fused_computation | loop fusion | bytes 4194320 | tf_op jit(solution)/shard_map/dynamic_slice | solution.py:231
  2.5 0.2 collective-permute-start.2
  2.6 1.3 %collective-permute-start = (bf16[512,512]{1,0:T(8,128)(2,1)S(1)}, bf16[512,512]{1,0:T(8,128)(2,1)S(1)}, u32[]{:S(2)}, u32[]{:S(2)}) collective-permute-start(bf16[512,512]{1,0:T(8,128)(2,1)S(1)} %get-tuple-element.6), channel_id=1, source_target_pairs={{0,1},{1,2},{2,3},{3,0},{4,5},{5,6},{6,7},{7,4},{8,9},{9,10},{10,1... | collective-permute-start | bytes 1572872 | tf_op jit(solution)/shard_map/ppermute | solution.py:236
  3.9 4.1 %collective-permute-start.1 = (bf16[512,512]{1,0:T(8,128)(2,1)S(1)}, bf16[512,512]{1,0:T(8,128)(2,1)S(1)}, u32[]{:S(2)}, u32[]{:S(2)}) collective-permute-start(bf16[512,512]{1,0:T(8,128)(2,1)S(1)} %get-tuple-element.8), channel_id=1, source_target_pairs={{0,2},{1,3},{2,0},{3,1},{4,6},{5,7},{6,4},{7,5},{8,10},{9,11},{10,... | collective-permute-start | bytes 1572872 | tf_op jit(solution)/shard_map/ppermute | solution.py:236
  8.0 21.7 %prefix.1.prior_ref = f32[4,2,128,128]{3,2,1,0:T(8,128)} custom-call(bf16[1024,512]{1,0:T(8,128)(2,1)} %k_ref.3, bf16[1024,512]{1,0:T(8,128)(2,1)} %v_ref.3, f32[4,1024]{1,0:T(4,128)} %bitcast.1), custom_call_target="tpu_custom_call" | custom-call | flops 536870912 | bytes 2097152 | tf_op jit(solution)/shard_map/prefix/pallas_call | solution.py:247
  29.7 37.3 %solve.1.r_ref = bf16[1024,512]{1,0:T(8,128)(2,1)} custom-call(bf16[1024,512]{1,0:T(8,128)(2,1)} %q_ref.1, bf16[1024,512]{1,0:T(8,128)(2,1)} %k_ref.3, bf16[1024,512]{1,0:T(8,128)(2,1)} %v_ref.3, f32[4,1024]{1,0:T(4,128)} %bitcast.2, f32[4]{0:T(128)} %ridge_ref.1, f32[4,2,128,128]{3,2,1,0:T(8,128)} %prefix.1.prior_ref), custom_call_target="tpu_custom_call" | custom-call | flops 7247757312 | bytes 4194304 | tf_op jit(solution)/shard_map/solve/pallas_call | solution.py:271
  67.0 0.0 collective-permute-done.2.refs_3_
  67.0 0.0 copy-start
  67.0 0.0 collective-permute-done.refs_1_
  67.0 0.0 copy-start.1
  67.0 0.0 collective-permute-done.1.refs_2_
  67.0 0.0 copy-start.2
  67.0 0.8 %copy-done = bf16[512,512]{1,0:T(8,128)(2,1)} copy-done((bf16[512,512]{1,0:T(8,128)(2,1)}, bf16[512,512]{1,0:T(8,128)(2,1)S(1)}, u32[]{:S(2)}) %copy-start) | copy-done | bytes 524312
  67.8 0.2 copy-done.1
  68.0 0.2 copy-done.2
  68.1 6.1 %project.1 = bf16[1,1024,2048]{2,1,0:T(8,128)(2,1)} custom-call(bf16[1024,512]{1,0:T(8,128)(2,1)} %solve.1.r_ref, bf16[512,512]{1,0:T(8,128)(2,1)} %get-tuple-element.7.refs_0_, bf16[512,512]{1,0:T(8,128)(2,1)} %copy-done.1, bf16[512,512]{1,0:T(8,128)(2,1)} %copy-done.2, bf16[512,512]{1,0:T(8,128)(2,1)} %copy-done), custom_call_target="tpu_custom_call" | custom-call | flops 2147483648 | bytes 4194304 | tf_op jit(solution)/shard_map/project/pallas_call | solution.py:300
Async XLA Ops:
  2.5 64.5 %collective-permute-start.2 = (bf16[512,512]{1,0:T(8,128)(2,1)S(1)}, bf16[512,512]{1,0:T(8,128)(2,1)S(1)}, u32[]{:S(2)}, u32[]{:S(2)}) collective-permute-start(bf16[512,512]{1,0:T(8,128)(2,1)S(1)} %get-tuple-element.5), channel_id=1, source_target_pairs={{0,3},{1,0},{2,1},{3,2},{4,7},{5,4},{6,5},{7,6},{8,11},{9,8},{10,9... | collective-permute-start | bytes 1572872 | tf_op jit(solution)/shard_map/ppermute | solution.py:236
  2.6 64.4 %collective-permute-start = (bf16[512,512]{1,0:T(8,128)(2,1)S(1)}, bf16[512,512]{1,0:T(8,128)(2,1)S(1)}, u32[]{:S(2)}, u32[]{:S(2)}) collective-permute-start(bf16[512,512]{1,0:T(8,128)(2,1)S(1)} %get-tuple-element.6), channel_id=1, source_target_pairs={{0,1},{1,2},{2,3},{3,0},{4,5},{5,6},{6,7},{7,4},{8,9},{9,10},{10,1... | collective-permute-start | bytes 1572872 | tf_op jit(solution)/shard_map/ppermute | solution.py:236
  3.9 63.1 %collective-permute-start.1 = (bf16[512,512]{1,0:T(8,128)(2,1)S(1)}, bf16[512,512]{1,0:T(8,128)(2,1)S(1)}, u32[]{:S(2)}, u32[]{:S(2)}) collective-permute-start(bf16[512,512]{1,0:T(8,128)(2,1)S(1)} %get-tuple-element.8), channel_id=1, source_target_pairs={{0,2},{1,3},{2,0},{3,1},{4,6},{5,7},{6,4},{7,5},{8,10},{9,11},{10,... | collective-permute-start | bytes 1572872 | tf_op jit(solution)/shard_map/ppermute | solution.py:236
  67.0 0.8 %copy-start = (bf16[512,512]{1,0:T(8,128)(2,1)}, bf16[512,512]{1,0:T(8,128)(2,1)S(1)}, u32[]{:S(2)}) copy-start(bf16[512,512]{1,0:T(8,128)(2,1)S(1)} %collective-permute-done.2.refs_3_) | copy-start | bytes 1572868
  67.0 1.0 %copy-start.1 = (bf16[512,512]{1,0:T(8,128)(2,1)}, bf16[512,512]{1,0:T(8,128)(2,1)S(1)}, u32[]{:S(2)}) copy-start(bf16[512,512]{1,0:T(8,128)(2,1)S(1)} %collective-permute-done.refs_1_) | copy-start | bytes 1572868
  67.0 1.1 %copy-start.2 = (bf16[512,512]{1,0:T(8,128)(2,1)}, bf16[512,512]{1,0:T(8,128)(2,1)S(1)}, u32[]{:S(2)}) copy-start(bf16[512,512]{1,0:T(8,128)(2,1)S(1)} %collective-permute-done.1.refs_2_) | copy-start | bytes 1572868
